TPU v7x, 128 devices: a whole 4x4x4 slice. The times are simulated.
128 devices in a mesh: vocab: 8 (over z, core), sample: 4 (over y), prompt: 4 (over x).
Axes of the slice: x: 4, y: 4, z: 4, core: 2. Of those that a mesh axis runs over, the one named last changes fastest.
Arguments:
- hidden: bfloat16 [1024, 4608], P(('sample', 'prompt'), 'vocab'), may hold values from -12 to 12
- gain: float32 [4608], replicated, may hold values from 0.25 to 1.75
- head: bfloat16 [4608, 256000], P(None, ('vocab', 'sample', 'prompt')), may hold values from -0.25 to 0.25
- candidates: int32 [32, 16], replicated, may hold values from 0 to 255999
- row_prompt: int32 [1024], replicated, may hold values from 0 to 31, as said below
Outputs:
- log_votes: float32 [32, 16], replicated
- row_lse: float32 [1024], P(('sample', 'prompt'))
Inputs may be any that keep to these rules, and one draw needn't show every extreme that they name: `row_prompt`: every prompt has at least one row; the rows of a prompt may stand anywhere among the 1024 rows.
All inputs are finite; a program needn't handle non-finite values.
Results may differ from a plain program's by a relative error of at most 0.00051.
Values may be sent and summed in bfloat16 or wider, within the bound.
No kernel may reach another device: no remote copies, remote signals or barrier semaphores. Data moves between devices by JAX's collectives and lax.ppermute only.
A program may use at most 128 MiB of HBM per device.

v0:
```python
import jax
import jax.numpy as jnp
from jax import lax
from jax.sharding import PartitionSpec as P

CAP = 30.0
EPS = 1e-06


def sent_to_all(array, axis):
    length = lax.axis_size(axis)
    return lax.all_to_all(
        jnp.broadcast_to(array[None], (length, *array.shape)), axis, 0, 0, tiled=True
    )


def over_copies(array, axis):
    return sent_to_all(array, axis).sum(axis=0)


def over_pieces(array, axis):
    parts = lax.all_gather(array, axis)
    return parts.sum(axis=0)


def body(hidden, gain, head, candidates, row_prompt):
    width = head.shape[0]
    vocab_dev = head.shape[1]
    shards = lax.axis_size("vocab")
    row_dev = hidden.shape[0]
    cols = hidden.shape[1]
    prompts = candidates.shape[0]
    xf = hidden.astype(jnp.float32)
    squared = over_copies(jnp.sum(xf * xf, axis=1), "vocab")
    scale = lax.rsqrt(squared / width + EPS)
    gain_part = lax.dynamic_slice_in_dim(gain, lax.axis_index("vocab") * cols, cols)
    normed = (xf * scale[:, None] * gain_part[None, :]).astype(jnp.bfloat16)
    pieces = lax.all_gather(normed[None], ("vocab", "sample", "prompt"), axis=0, tiled=True)
    groups = pieces.shape[0] // shards
    pieces = pieces.reshape(shards, groups, row_dev, cols)
    weight = head.reshape(shards, cols, vocab_dev)
    raw = jnp.einsum("vgrd,vdc->grc", pieces, weight, preferred_element_type=jnp.float32)
    logits = CAP * jnp.tanh(raw.reshape(groups * row_dev, vocab_dev) / CAP)
    rows = logits.shape[0]
    exps = jnp.exp(logits)
    sumexp = jnp.sum(exps, axis=1)
    onehot = (row_prompt[:, None] == jnp.arange(prompts, dtype=jnp.int32)[None, :]).astype(
        jnp.float32
    )
    cands = candidates.shape[1]
    offset = lax.axis_index(("vocab", "sample", "prompt")) * vocab_dev
    cand_local = candidates - offset
    columns = jnp.arange(vocab_dev, dtype=jnp.int32)
    selector = (columns[:, None, None] == cand_local[None, :, :]).astype(jnp.float32)
    selector = selector.reshape(vocab_dev, prompts * cands)
    matched = jnp.dot(
        exps, selector, precision=lax.Precision.HIGHEST, preferred_element_type=jnp.float32
    )
    numer = jnp.einsum(
        "rpc,rp->rc",
        matched.reshape(rows, prompts, cands),
        onehot,
        precision=lax.Precision.HIGHEST,
        preferred_element_type=jnp.float32,
    )
    group = lax.axis_index(("sample", "prompt"))
    totals, numers = (
        over_pieces(sumexp, ("vocab", "sample", "prompt")),
        over_pieces(numer, ("vocab", "sample", "prompt")),
    )
    prob = numers / totals[:, None]
    tally = jnp.dot(
        onehot.T, prob, precision=lax.Precision.HIGHEST, preferred_element_type=jnp.float32
    )
    row_lse = lax.dynamic_slice_in_dim(jnp.log(totals), group * row_dev, row_dev, 0)
    return (jnp.log(tally), row_lse)


def solution(mesh):
    placed = (
        P(("sample", "prompt"), "vocab"),
        P(),
        P(None, ("vocab", "sample", "prompt")),
        P(),
        P(),
    )
    return jax.shard_map(
        body, mesh=mesh, in_specs=placed, out_specs=(P(), P(("sample", "prompt"))), check_vma=False
    )
```

profile of v0, /device:TPU:1, one launch (start us, length us, event | category | flops | bytes accessed | tf_op | source)
XLA Modules:
  0.0 215.8 jit_solution(7561266731137708748)
XLA Ops:
  7.2 1.0 fusion.14
  8.2 0.6 broadcast_in_dim.4
  8.8 6.8 %all-to-all-start = ((f32[8,1,64]{2,1,0:T(1,128)}), f32[8,1,64]{2,1,0:T(1,128)S(1)}, u32[]{:S(2)}, u32[]{:S(2)}) async-start(f32[8,1,64]{2,1,0:T(1,128)} %broadcast_in_dim.4), calls=%async_computation | async-start | bytes 8192 | tf_op jit(solution)/shard_map/all_to_all | solution.py:12
  15.6 0.8 dynamic_slice.6
  16.4 3.8 %all-to-all-done = f32[8,1,64]{2,1,0:T(1,128)S(1)} async-done(((f32[8,1,64]{2,1,0:T(1,128)}), f32[8,1,64]{2,1,0:T(1,128)S(1)}, u32[]{:S(2)}, u32[]{:S(2)}) %all-to-all-start) | async-done | bytes 2080 | tf_op jit(solution)/shard_map/all_to_all | solution.py:12
  20.1 1.6 fusion.16
  21.8 0.0 all-gather.6.cloned.1.call-update
  21.8 0.0 copy-start.1
  21.8 0.0 copy-start
  21.8 0.0 all-gather.8.cloned.1.call-start
  21.8 24.8 %copy.23 = bf16[4608,2000]{1,0:T(8,128)(2,1)} copy(bf16[4608,2000]{0,1:T(8,128)(2,1)} %param.7) | data formatting | bytes 36864000 | tf_op args[2]
  46.6 0.2 fusion.12
  46.8 0.2 copy.33
  47.0 46.3 %all-gather.6.cloned.1.call-done = bf16[8192,576]{1,0:T(8,128)(2,1)} async-done(((bf16[64,576]{1,0:T(8,128)(2,1)}), bf16[8192,576]{1,0:T(8,128)(2,1)}) %all-gather.6.cloned.1.call-update) | async-done | bytes 9437200 | tf_op jit(solution)/shard_map/all_gather | solution.py:38
  93.3 27.7 %fusion.5 = (f32[1024]{0:T(1024)S(1)}, f32[1024,2000,1]{0,1,2:T(8,128)S(1)}) fusion(bf16[1024,576,8]{1,0,2:T(8,128)(2,1)} %bitcast.37, bf16[8,576,2000]{2,1,0:T(8,128)(2,1)} %bitcast.34), kind=kOutput, calls=%fused_computation.7 | convolution fusion | flops 18880512000 | bytes 36065280 | tf_op jit(solution)/shard_map/vgrd,vdc->grc/dot_general | solution.py:42
  121.0 9.4 %multiply_reduce_fusion = f32[1024,16]{0,1:T(8,128)} fusion(f32[1024,32]{0,1:T(8,128)S(1)} %copy.33, s32[32,16]{0,1:T(8,128)S(1)} %broadcast_subtract_fusion, f32[1024,2000,1]{0,1,2:T(8,128)S(1)} %get-tuple-element.3), kind=kOutput, calls=%fused_computation.11 | convolution fusion | flops 12589064192 | bytes 8390656 | tf_op jit(solution)/shard_map/dot_general | solution.py:56
  130.4 0.0 all-gather.8.cloned.1.call-update
  130.5 55.7 %all-gather.2 = f32[131072]{0:T(1024)S(1)} all-gather(f32[1024]{0:T(1024)S(1)} %get-tuple-element.2), channel_id=4, replica_groups=mesh['vocab'=8,'sample'=4,'prompt'=4] {'vocab','sample','prompt'}, dimensions={0}, use_global_device_ids=true | all-gather | bytes 528384 | tf_op jit(solution)/shard_map/all_gather | solution.py:22
  186.1 0.1 reshape.42
  186.3 0.6 dynamic_slice.7
  186.9 11.8 %all-gather.8.cloned.1.call-done = f32[131072,16]{0,1:T(8,128)} async-done(((f32[1024,16]{0,1:T(8,128)}), f32[131072,16]{0,1:T(8,128)}) %all-gather.8.cloned.1.call-update) | async-done | bytes 8388624 | tf_op jit(solution)/shard_map/all_gather | solution.py:22
  198.6 8.2 %copy.35 = f32[2,8,128,1024]{3,2,1,0:T(8,128)S(1)} copy(f32[2,8,128,1024]{3,1,2,0:T(8,128)} %bitcast.35) | data formatting | bytes 16777216
  206.9 1.1 bitcast_reduce_fusion
  207.9 1.0 convolution_log_fusion
  (8 shorter events, 0.1 us)
Async XLA Ops:
  8.8 11.3 %all-to-all-start = ((f32[8,1,64]{2,1,0:T(1,128)}), f32[8,1,64]{2,1,0:T(1,128)S(1)}, u32[]{:S(2)}, u32[]{:S(2)}) async-start(f32[8,1,64]{2,1,0:T(1,128)} %broadcast_in_dim.4), calls=%async_computation | async-start | bytes 8192 | tf_op jit(solution)/shard_map/all_to_all | solution.py:12
  15.6 77.7 %all-gather.6.cloned.1.call-start = ((), (), s32[]{:S(2)}) async-start(), calls=%async_computation.1 | async-start | bytes 10567680 | tf_op jit(solution)/shard_map/all_gather | solution.py:38
  21.8 24.9 %copy-start.1 = (s32[1024]{0:T(1024)S(1)}, s32[1024]{0:T(1024)}, u32[]{:S(2)}) copy-start(s32[1024]{0:T(1024)} %param.9) | copy-start | bytes 12292
  21.8 25.2 %copy-start = (s32[32,16]{0,1:T(8,128)S(1)}, s32[32,16]{0,1:T(8,128)}, u32[]{:S(2)}) copy-start(s32[32,16]{0,1:T(8,128)} %param.8) | copy-start | bytes 6148
  21.8 176.8 %all-gather.8.cloned.1.call-start = ((), (), s32[]{:S(2)}) async-start(), calls=%async_computation.2 | async-start | bytes 8454144 | tf_op jit(solution)/shard_map/all_gather | solution.py:22
Sparse Core Ops, SparseCore 0:
  21.9 71.3 all-gather.5
  130.6 68.0 all-gather.7
where the time goes:
time: 217 us; the launch traced here: 216 us
  waiting for transfers between devices  61.8 us (28%)
  blocking collectives  55.7 us (26%)
  matrix products  38.1 us (18%)
  local copies, waits for them, and re-layouts  35.3 us (16%)
  between operations  14.1 us (6%)
  starting transfers between devices  6.85 us (3%)
  other arithmetic  3.95 us (2%)
    all_gather x1, blocking collectives, over_pieces(): parts = lax.all_gather(array, axis)  55.7 us
    all_gather x1, waiting for transfers between devices, body(): lax.all_gather(normed[None], ('vocab', 'sample', 'prompt'), axis=0, tiled...  46.3 us
    unnamed x7, local copies, waits for them, and re-layouts  33.2 us
    dot_general x1, matrix products, body(): jnp.einsum('vgrd,vdc->grc', pieces, weight, preferred_element_type=jnp.fl...  27.7 us
    all_gather x1, waiting for transfers between devices, over_pieces(): parts = lax.all_gather(array, axis)  11.8 us
    dot_general x1, matrix products, body(): jnp.dot(exps, selector, precision=lax.Precision.HIGHEST, preferred_elemen...  9.41 us
    all_to_all x1, starting transfers between devices, sent_to_all(): lax.all_to_all(jnp.broadcast_to(array[None], (length, *array.shape)), axi...  6.8 us
  transfers between devices with their start and end apart: 3, of which 3 were waited for; matrix products, arithmetic and copies ran while one was open for 12% of the time, Pallas kernels for 0%

commit v1 on v0

--- a/solution.py
+++ b/solution.py
@@ -35,7 +35,9 @@
     scale = lax.rsqrt(squared / width + EPS)
     gain_part = lax.dynamic_slice_in_dim(gain, lax.axis_index("vocab") * cols, cols)
     normed = (xf * scale[:, None] * gain_part[None, :]).astype(jnp.bfloat16)
-    pieces = lax.all_gather(normed[None], ("vocab", "sample", "prompt"), axis=0, tiled=True)
+    own = normed[None]
+    outgoing = jnp.stack([own] * lax.axis_size(("vocab", "sample", "prompt")))
+    pieces = jnp.concatenate(lax.all_to_all(outgoing, ("vocab", "sample", "prompt"), 0, 0), axis=0)
     groups = pieces.shape[0] // shards
     pieces = pieces.reshape(shards, groups, row_dev, cols)
     weight = head.reshape(shards, cols, vocab_dev)

time: 217 us -> 302 us (1.39)
  waiting for transfers between devices: 61.8 us -> 118 us
  blocking collectives: 55.7 us -> 71.2 us
  starting transfers between devices: 6.85 us -> 15.1 us
  local copies, waits for them, and re-layouts: 35.3 us -> 40.7 us
    all_to_all x0 -> x1, waiting for transfers between devices: none -> 98.8 us  [body(): lax.all_to_all(outgoing, ('vocab', 'sample', 'prompt'), 0, 0)]
    all_gather x1 -> x0, waiting for transfers between devices: 46.3 us -> none  [body(): lax.all_gather(normed[None], ('vocab', 'sample', 'prompt'), axis=0, tiled...]
    all_gather x1, blocking collectives: 55.7 us -> 71.2 us  [over_pieces(): parts = lax.all_gather(array, axis)]
    all_to_all x0 -> x1, starting transfers between devices: none -> 8.22 us  [body(): lax.all_to_all(outgoing, ('vocab', 'sample', 'prompt'), 0, 0)]
    another operation x0 -> x1, local copies, waits for them, and re-layouts: none -> 5.45 us  [body(): outgoing = jnp.stack([own] * lax.axis_size(('vocab', 'sample', 'prompt')))]
    all_gather x1, waiting for transfers between devices: 11.8 us -> 15.5 us  [over_pieces(): parts = lax.all_gather(array, axis)]
  transfers between devices with their start and end apart: 3 -> 3, of which waited for: 3 -> 3; matrix products, arithmetic and copies ran while one was open for 12% -> 9% of each run, Pallas kernels for 0% -> 0%
where the time goes in v1:
time: 302 us; the launch traced here: 301 us
  waiting for transfers between devices  118 us (39%)
  blocking collectives  71.2 us (24%)
  local copies, waits for them, and re-layouts  40.7 us (13%)
  matrix products  38.1 us (13%)
  starting transfers between devices  15.1 us (5%)
  between operations  14.1 us (5%)
  other arithmetic  3.31 us (1%)
    all_to_all x1, waiting for transfers between devices, body(): lax.all_to_all(outgoing, ('vocab', 'sample', 'prompt'), 0, 0)  98.8 us
    all_gather x1, blocking collectives, over_pieces(): parts = lax.all_gather(array, axis)  71.2 us
    unnamed x7, local copies, waits for them, and re-layouts  33.2 us
    dot_general x1, matrix products, body(): jnp.einsum('vgrd,vdc->grc', pieces, weight, preferred_element_type=jnp.fl...  27.7 us
    all_gather x1, waiting for transfers between devices, over_pieces(): parts = lax.all_gather(array, axis)  15.5 us
    dot_general x1, matrix products, body(): jnp.dot(exps, selector, precision=lax.Precision.HIGHEST, preferred_elemen...  9.38 us
    all_to_all x1, starting transfers between devices, body(): lax.all_to_all(outgoing, ('vocab', 'sample', 'prompt'), 0, 0)  8.22 us
    all_to_all x1, starting transfers between devices, sent_to_all(): lax.all_to_all(jnp.broadcast_to(array[None], (length, *array.shape)), axi...  6.8 us
  transfers between devices with their start and end apart: 3, of which 3 were waited for; matrix products, arithmetic and copies ran while one was open for 9% of the time, Pallas kernels for 0%

profile of v1, /device:TPU:1, one launch (start us, length us, event | category | flops | bytes accessed | tf_op | source)
XLA Modules:
  0.0 300.5 jit_solution(8129218607477149020)
XLA Ops:
  7.2 1.0 fusion.14
  8.2 0.6 broadcast_in_dim.2
  8.8 6.8 %all-to-all-start = ((f32[8,1,64]{2,1,0:T(1,128)}), f32[8,1,64]{2,1,0:T(1,128)S(1)}, u32[]{:S(2)}, u32[]{:S(2)}) async-start(f32[8,1,64]{2,1,0:T(1,128)} %broadcast_in_dim.2), calls=%async_computation | async-start | bytes 8192 | tf_op jit(solution)/shard_map/all_to_all | solution.py:12
  15.6 0.8 dynamic_slice.6
  16.4 3.8 %all-to-all-done = f32[8,1,64]{2,1,0:T(1,128)S(1)} async-done(((f32[8,1,64]{2,1,0:T(1,128)}), f32[8,1,64]{2,1,0:T(1,128)S(1)}, u32[]{:S(2)}, u32[]{:S(2)}) %all-to-all-start) | async-done | bytes 2080 | tf_op jit(solution)/shard_map/all_to_all | solution.py:12
  20.1 1.0 fusion.16
  21.1 5.4 %stack.3 = bf16[128,1,64,576]{3,2,1,0:T(8,128)(2,1)} broadcast(bf16[64,576]{1,0:T(8,128)(2,1)S(1)} %fusion.16), dimensions={2,3} | broadcast | bytes 9510912 | tf_op jit(solution)/shard_map/stack | solution.py:39
  26.6 8.2 %all-to-all-start.1 = ((bf16[128,1,64,576]{3,2,1,0:T(8,128)(2,1)}), bf16[128,1,64,576]{3,2,1,0:T(8,128)(2,1)}, u32[]{:S(2)}, u32[]{:S(2)}) async-start(bf16[128,1,64,576]{3,2,1,0:T(8,128)(2,1)} %stack.3), calls=%async_computation.1 | async-start | bytes 20971520 | tf_op jit(solution)/shard_map/all_to_all | solution.py:40
  34.8 0.0 copy-start.1
  34.8 0.0 all-gather.4.cloned.1.call-start
  34.9 24.7 %copy.22 = bf16[4608,2000]{1,0:T(8,128)(2,1)} copy(bf16[4608,2000]{0,1:T(8,128)(2,1)} %param.7) | data formatting | bytes 36864000 | tf_op args[2]
  59.6 0.2 fusion.12
  59.8 0.2 copy.33
  60.0 98.8 %all-to-all-done.1 = bf16[128,1,64,576]{3,2,1,0:T(8,128)(2,1)} async-done(((bf16[128,1,64,576]{3,2,1,0:T(8,128)(2,1)}), bf16[128,1,64,576]{3,2,1,0:T(8,128)(2,1)}, u32[]{:S(2)}, u32[]{:S(2)}) %all-to-all-start.1) | async-done | bytes 9437216 | tf_op jit(solution)/shard_map/all_to_all | solution.py:40
  158.8 27.7 %fusion.5 = (f32[1024]{0:T(1024)S(1)}, f32[1024,2000,1]{0,1,2:T(8,128)S(1)}) fusion(bf16[1024,576,8]{1,0,2:T(8,128)(2,1)} %bitcast.3, bf16[8,576,2000]{2,1,0:T(8,128)(2,1)} %bitcast.34), kind=kOutput, calls=%fused_computation.7 | convolution fusion | flops 18880512000 | bytes 36065280 | tf_op jit(solution)/shard_map/vgrd,vdc->grc/dot_general | solution.py:44
  186.5 9.4 %multiply_reduce_fusion = f32[1024,16]{0,1:T(8,128)} fusion(f32[1024,32]{0,1:T(8,128)S(1)} %copy.33, s32[32,16]{0,1:T(8,128)S(1)} %broadcast_subtract_fusion, f32[1024,2000,1]{0,1,2:T(8,128)S(1)} %get-tuple-element.3), kind=kOutput, calls=%fused_computation.11 | convolution fusion | flops 12589064192 | bytes 8390656 | tf_op jit(solution)/shard_map/dot_general | solution.py:58
  195.9 0.0 all-gather.4.cloned.1.call-update
  195.9 71.2 %all-gather.1 = f32[131072]{0:T(1024)S(1)} all-gather(f32[1024]{0:T(1024)S(1)} %get-tuple-element.2), channel_id=3, replica_groups=mesh['vocab'=8,'sample'=4,'prompt'=4] {'vocab','sample','prompt'}, dimensions={0}, use_global_device_ids=true | all-gather | bytes 528384 | tf_op jit(solution)/shard_map/all_gather | solution.py:22
  267.1 0.1 reshape.39
  267.3 0.6 dynamic_slice.7
  267.9 15.5 %all-gather.4.cloned.1.call-done = f32[131072,16]{0,1:T(8,128)} async-done(((f32[1024,16]{0,1:T(8,128)}), f32[131072,16]{0,1:T(8,128)}) %all-gather.4.cloned.1.call-update) | async-done | bytes 8388624 | tf_op jit(solution)/shard_map/all_gather | solution.py:22
  283.4 8.2 %copy.35 = f32[2,8,128,1024]{3,2,1,0:T(8,128)S(1)} copy(f32[2,8,128,1024]{3,1,2,0:T(8,128)} %bitcast.35) | data formatting | bytes 16777216
  291.6 1.1 bitcast_reduce_fusion
  292.7 1.0 convolution_log_fusion
  (8 shorter events, 0.1 us)
Async XLA Ops:
  8.8 11.3 %all-to-all-start = ((f32[8,1,64]{2,1,0:T(1,128)}), f32[8,1,64]{2,1,0:T(1,128)S(1)}, u32[]{:S(2)}, u32[]{:S(2)}) async-start(f32[8,1,64]{2,1,0:T(1,128)} %broadcast_in_dim.2), calls=%async_computation | async-start | bytes 8192 | tf_op jit(solution)/shard_map/all_to_all | solution.py:12
  26.6 132.2 %all-to-all-start.1 = ((bf16[128,1,64,576]{3,2,1,0:T(8,128)(2,1)}), bf16[128,1,64,576]{3,2,1,0:T(8,128)(2,1)}, u32[]{:S(2)}, u32[]{:S(2)}) async-start(bf16[128,1,64,576]{3,2,1,0:T(8,128)(2,1)} %stack.3), calls=%async_computation.1 | async-start | bytes 20971520 | tf_op jit(solution)/shard_map/all_to_all | solution.py:40
  34.8 24.8 %copy-start.1 = (s32[1024]{0:T(1024)S(1)}, s32[1024]{0:T(1024)}, u32[]{:S(2)}) copy-start(s32[1024]{0:T(1024)} %param.9) | copy-start | bytes 12292
  34.8 25.2 %copy-start = (s32[32,16]{0,1:T(8,128)S(1)}, s32[32,16]{0,1:T(8,128)}, u32[]{:S(2)}) copy-start(s32[32,16]{0,1:T(8,128)} %param.8) | copy-start | bytes 6148
  34.8 248.6 %all-gather.4.cloned.1.call-start = ((), (), s32[]{:S(2)}) async-start(), calls=%async_computation.2 | async-start | bytes 8454144 | tf_op jit(solution)/shard_map/all_gather | solution.py:22
Sparse Core Ops, SparseCore 0:
  196.0 87.3 all-gather.3
